TPU v7x, 32 devices: a whole 2x2x4 slice. The times are simulated.
32 devices in a mesh: grp: 4 (over y, x), own: 8 (over z, core).
Axes of the slice: x: 2, y: 2, z: 4, core: 2. Of those that a mesh axis runs over, the one named last changes fastest.
Arguments:
- grad_parts: float32 [4, 8, 4, 8, 16, 2, 128], P('grp', 'own'), may hold values from -6 to 6
- block_ids: int32 [8, 4, 8, 16], P('own'), may hold values from 0 to 8191, as said below
- block_counts: int32 [8, 4, 8], P('own'), may hold values from 0 to 16, as said below
- params: float32 [8, 32768, 2, 128], P(None, ('grp', 'own')), may hold values from -4 to 4
- first_moment: float32 [8, 32768, 2, 128], P(None, ('grp', 'own')), may hold values from -2 to 2
- second_moment: float32 [8, 32768, 2, 128], P(None, ('grp', 'own')), may hold values from 0.0001 to 0.03
Outputs:
- new_params: float32 [8, 32768, 2, 128], P(None, ('grp', 'own'))
- new_first: float32 [8, 32768, 2, 128], P(None, ('grp', 'own'))
- new_second: float32 [8, 32768, 2, 128], P(None, ('grp', 'own'))
Inputs may be any that keep to these rules, and one draw needn't show every extreme that they name: `block_ids`: within one row (fixed group and destination) the 16 block numbers are distinct; numbers in slots beyond the count are arbitrary but in range. `block_counts`: some destination device gets 16 used slots from every ray group.
All inputs are finite; a program needn't handle non-finite values.
Results may differ from a plain program's by a relative error of at most 0.00002.
Values sent between devices are 32-bit elements; how exact they have to be, the bound alone decides.
A program may use at most 128 MiB of HBM per device.

v0:
```python
import jax
import jax.numpy as jnp
from jax import lax
from jax.sharding import PartitionSpec as P


def shards(grad_parts, block_ids, block_counts, params, first_moment, second_moment):
    member = lax.axis_index("grp")
    partial_value = grad_parts[0, 0]
    listing = block_ids[0]
    tallies = block_counts[0]
    share = lax.psum_scatter(partial_value, "grp", scatter_dimension=0, tiled=True)[0]
    send_ids = lax.dynamic_index_in_dim(listing, member, 0, keepdims=False)
    send_counts = lax.dynamic_index_in_dim(tallies, member, 0, keepdims=False)
    summed, mine_ids, mine_counts = (
        lax.all_to_all(share, "own", split_axis=0, concat_axis=0, tiled=True),
        lax.all_to_all(send_ids, "own", split_axis=0, concat_axis=0, tiled=True),
        lax.all_to_all(send_counts, "own", split_axis=0, concat_axis=0, tiled=True),
    )
    slot_count = summed.shape[1]
    width = summed.shape[2] * summed.shape[3]
    local_blocks = params.shape[0] * params.shape[1]
    valid = jnp.arange(slot_count, dtype=jnp.int32)[None, :] < mine_counts[:, None]
    rows = summed.reshape(-1, width) * valid.reshape(-1, 1).astype(jnp.float32)
    target = mine_ids.reshape(-1).astype(jnp.int32)
    dense = jax.ops.segment_sum(rows, target, num_segments=local_blocks)
    hits = (
        jax.ops.segment_sum(valid.reshape(-1).astype(jnp.int32), target, num_segments=local_blocks)
        > 0
    )
    square = jnp.sum(dense * dense)
    touched = jnp.sum(hits.astype(jnp.float32))
    square, touched = lax.psum((square, touched), ("grp", "own"))
    rms = jnp.sqrt(square / (touched * width) + 1e-06)
    scale = jnp.minimum(jnp.float32(1.0), 0.5 / rms)
    clipped = scale * dense
    old_p = params.reshape(local_blocks, width)
    old_m = first_moment.reshape(local_blocks, width)
    old_v = second_moment.reshape(local_blocks, width)
    mask = hits[:, None]
    new_m = jnp.where(mask, 0.9 * old_m + 0.1 * clipped, old_m)
    new_v = jnp.where(mask, 0.99 * old_v + 0.01 * clipped * clipped, old_v)
    stepped = old_p - 0.01 * (new_m / (1.0 - 0.9**8)) / (jnp.sqrt(new_v / (1.0 - 0.99**8)) + 1e-08)
    new_p = jnp.where(mask, stepped, old_p)
    shape = params.shape
    return (new_p.reshape(shape), new_m.reshape(shape), new_v.reshape(shape))


def solution(mesh):
    in_specs = (
        P("grp", "own", None, None, None, None, None),
        P("own", None, None, None),
        P("own", None, None),
        P(None, ("grp", "own"), None, None),
        P(None, ("grp", "own"), None, None),
        P(None, ("grp", "own"), None, None),
    )
    out_specs = (
        P(None, ("grp", "own"), None, None),
        P(None, ("grp", "own"), None, None),
        P(None, ("grp", "own"), None, None),
    )
    return jax.shard_map(shards, mesh=mesh, in_specs=in_specs, out_specs=out_specs, check_vma=False)
```

profile of v0, /device:TPU:0, one launch (start us, length us, event | category | flops | bytes accessed | tf_op | source)
XLA Modules:
  0.0 161.3 jit_solution(8497231740222353141)
XLA Ops:
  7.2 0.0 copy-start
  7.2 0.0 reduce-scatter.4.cloned.1.call-start
  7.2 1.9 %copy.30 = f32[1,1,4,8,16,2,128]{6,4,5,3,2,1,0:T(8,128)} copy(f32[1,1,4,8,16,2,128]{6,5,4,3,2,1,0:T(2,128)} %param.6) | data formatting | bytes 1048576 | tf_op args[0]
  9.1 0.0 reduce-scatter.4.cloned.1.call-update
  9.1 0.7 dynamic-slice_bitcast_fusion
  9.8 0.7 copy.13
  10.5 6.4 %all-to-all-start.1 = ((s32[8,1,1]{2,1,0:T(1,128)}), s32[8,1,1]{2,1,0:T(1,128)S(1)}, u32[]{:S(2)}, u32[]{:S(2)}) async-start(s32[8,1,1]{2,1,0:T(1,128)} %copy.13), calls=%async_computation.1 | async-start | bytes 8192 | tf_op jit(solution)/shard_map/all_to_all | solution.py:18
  16.8 0.0 copy-done
  16.9 0.6 constant_dynamic-slice_fusion
  17.5 4.9 %all-to-all-done.1 = s32[8,1,1]{2,1,0:T(1,128)S(1)} async-done(((s32[8,1,1]{2,1,0:T(1,128)}), s32[8,1,1]{2,1,0:T(1,128)S(1)}, u32[]{:S(2)}, u32[]{:S(2)}) %all-to-all-start.1) | async-done | bytes 64 | tf_op jit(solution)/shard_map/all_to_all | solution.py:18
  22.4 3.3 %all-to-all-start = ((s32[8,1,16]{2,1,0:T(1,128)}), s32[8,1,16]{2,1,0:T(1,128)S(1)}, u32[]{:S(2)}, u32[]{:S(2)}) async-start(s32[8,1,16]{2,1,0:T(1,128)} %bitcast.1), calls=%async_computation | async-start | bytes 8192 | tf_op jit(solution)/shard_map/all_to_all | solution.py:17
  25.7 0.2 reduce.1
  25.9 5.2 %all-to-all-done = s32[8,1,16]{2,1,0:T(1,128)S(1)} async-done(((s32[8,1,16]{2,1,0:T(1,128)}), s32[8,1,16]{2,1,0:T(1,128)S(1)}, u32[]{:S(2)}, u32[]{:S(2)}) %all-to-all-start) | async-done | bytes 544 | tf_op jit(solution)/shard_map/all_to_all | solution.py:17
  31.1 8.1 %reduce-scatter.4.cloned.1.call-done = f32[1,8,16,2,128]{4,2,3,1,0:T(8,128)} async-done(((f32[4,8,16,2,128]{4,2,3,1,0:T(8,128)}), f32[1,8,16,2,128]{4,2,3,1,0:T(8,128)}) %reduce-scatter.4.cloned.1.call-update) | async-done | bytes 131088
  39.2 4.6 %all-to-all-start.2 = ((f32[8,16,2,128]{3,1,2,0:T(8,128)}), f32[8,16,2,128]{3,1,2,0:T(8,128)S(1)}, u32[]{:S(2)}, u32[]{:S(2)}) async-start(f32[8,16,2,128]{3,1,2,0:T(8,128)} %bitcast.42), calls=%async_computation.2 | async-start | bytes 262144 | tf_op jit(solution)/shard_map/all_to_all | solution.py:16
  43.8 0.1 fusion.10
  43.9 0.1 reshape.72
  44.0 0.1 reshape.77
  44.1 0.5 broadcast.24
  44.6 0.7 reduce.4
  45.3 0.1 reshape.75
  45.3 1.3 scatter_custom_fusion
  46.6 0.6 convert_reduce_fusion
  47.2 3.4 %all-to-all-done.2 = f32[8,16,2,128]{3,1,2,0:T(8,128)S(1)} async-done(((f32[8,16,2,128]{3,1,2,0:T(8,128)}), f32[8,16,2,128]{3,1,2,0:T(8,128)S(1)}, u32[]{:S(2)}, u32[]{:S(2)}) %all-to-all-start.2) | async-done | bytes 131104 | tf_op jit(solution)/shard_map/all_to_all | solution.py:16
  50.6 0.1 copy.15
  50.7 5.2 %scatter_custom_fusion.1 = f32[8192,256]{1,0:T(8,128)} fusion(s32[128]{0:T(128)S(1)} %reshape.75, f32[]{:T(128)} %constant.20.clone.1, f32[16,8,2,128]{3,2,1,0:T(2,128)S(1)} %bitcast.41, f32[128]{0:T(128)S(1)} %reshape.72), kind=kCustom, calls=%fused_computation.11 | custom fusion | flops 65536 | bytes 8520196 | tf_op jit(solution)/shard_map/scatter-add | solution.py:26
  55.9 6.1 %multiply_reduce_fusion = f32[]{:T(128)} fusion(f32[8192,256]{1,0:T(8,128)} %scatter_custom_fusion.1), kind=kLoop, calls=%fused_computation.10 | loop fusion | flops 4194303 | bytes 8388612 | tf_op jit(solution)/shard_map/reduce_sum | solution.py:31
  62.0 38.8 %all-reduce.1 = (f32[]{:T(128)}, f32[]{:T(128)}) all-reduce(f32[]{:T(128)} %multiply_reduce_fusion, f32[]{:T(128)} %get-tuple-element.8), channel_id=1, replica_groups=mesh['grp'=4,'own'=8] {'grp','own'}, use_global_device_ids=true, to_apply=%region_4.5 | all-reduce | flops 2 | bytes 16 | tf_op jit(solution)/shard_map/psum | solution.py:33
  102.2 20.0 %subtract_select_fusion = (f32[8192,256]{1,0:T(8,128)}, f32[8192,256]{1,0:T(8,128)}, f32[8192,256]{1,0:T(8,128)}) fusion(f32[1024,8,2,128]{3,2,1,0:T(2,128)} %bitcast.37, pred[8192]{0:T(1024)(128)(4,1)S(1)} %get-tuple-element.9, f32[8192,256]{1,0:T(8,128)} %scatter_custom_fusion.1, f32[]{:T(128)S(6)} %min_shard_map.3, f32[1024,8,2,128]{3,2,1,0:T(2,128)} %bitcast.38, ...), kind=kLoop, calls=%fused_computation.2 | loop fusion | flops 33554432 | bytes 58728452 | tf_op jit(solution)/shard_map/jit(_where)/select_n | solution.py:44
  122.2 10.8 %reshape.68 = f32[8,1024,2,128]{3,2,1,0:T(2,128)} reshape(f32[8192,256]{1,0:T(8,128)} %get-tuple-element.5) | data formatting | bytes 16777216 | tf_op jit(solution)/shard_map/reshape | solution.py:46
  133.0 10.8 %reshape.69 = f32[8,1024,2,128]{3,2,1,0:T(2,128)} reshape(f32[8192,256]{1,0:T(8,128)} %get-tuple-element.6) | data formatting | bytes 16777216 | tf_op jit(solution)/shard_map/reshape | solution.py:46
  143.7 0.0 copy-start.1
  143.7 10.8 %reshape.70 = f32[8,1024,2,128]{3,2,1,0:T(2,128)} reshape(f32[8192,256]{1,0:T(8,128)} %get-tuple-element.7) | data formatting | bytes 16777216 | tf_op jit(solution)/shard_map/reshape | solution.py:46
  154.5 0.0 copy-done.1
Async XLA Ops:
  7.2 9.7 %copy-start = (s32[1,4,8,16]{3,2,1,0:T(8,128)S(1)}, s32[1,4,8,16]{3,2,1,0:T(8,128)}, u32[]{:S(2)}) copy-start(s32[1,4,8,16]{3,2,1,0:T(8,128)} %param.7) | copy-start | bytes 6148
  7.2 32.0 %reduce-scatter.4.cloned.1.call-start = ((), (), s32[]{:S(2)}) async-start(), calls=%async_computation.4 | async-start | bytes 655360
  10.5 11.9 %all-to-all-start.1 = ((s32[8,1,1]{2,1,0:T(1,128)}), s32[8,1,1]{2,1,0:T(1,128)S(1)}, u32[]{:S(2)}, u32[]{:S(2)}) async-start(s32[8,1,1]{2,1,0:T(1,128)} %copy.13), calls=%async_computation.1 | async-start | bytes 8192 | tf_op jit(solution)/shard_map/all_to_all | solution.py:18
  22.4 8.8 %all-to-all-start = ((s32[8,1,16]{2,1,0:T(1,128)}), s32[8,1,16]{2,1,0:T(1,128)S(1)}, u32[]{:S(2)}, u32[]{:S(2)}) async-start(s32[8,1,16]{2,1,0:T(1,128)} %bitcast.1), calls=%async_computation | async-start | bytes 8192 | tf_op jit(solution)/shard_map/all_to_all | solution.py:17
  39.2 11.4 %all-to-all-start.2 = ((f32[8,16,2,128]{3,1,2,0:T(8,128)}), f32[8,16,2,128]{3,1,2,0:T(8,128)S(1)}, u32[]{:S(2)}, u32[]{:S(2)}) async-start(f32[8,16,2,128]{3,1,2,0:T(8,128)} %bitcast.42), calls=%async_computation.2 | async-start | bytes 262144 | tf_op jit(solution)/shard_map/all_to_all | solution.py:16
  143.7 10.8 %copy-start.1 = (s32[1,4,8,16]{3,2,1,0:T(8,128)S(1)}, s32[1,4,8,16]{3,2,1,0:T(8,128)}, u32[]{:S(2)}) copy-start(s32[1,4,8,16]{3,2,1,0:T(8,128)} %param.7) | copy-start | bytes 6148
Sparse Core Ops, SparseCore 0:
  11.4 27.8 reduce-scatter.3
where the time goes:
time: 162 us; the launch traced here: 161 us
  blocking collectives  38.8 us (24%)
  local copies, waits for them, and re-layouts  37 us (23%)
  other arithmetic  34.2 us (21%)
  waiting for transfers between devices  21.6 us (13%)
  between operations  15.4 us (10%)
  starting transfers between devices  14.3 us (9%)
    psum x1, blocking collectives, shards(): square, touched = lax.psum((square, touched), ('grp', 'own'))  38.8 us
    reshape x3, local copies, waits for them, and re-layouts, shards(): return (new_p.reshape(shape), new_m.reshape(shape), new_v.reshape(shape))  32.3 us
    select_n x1, other arithmetic, shards(): new_p = jnp.where(mask, stepped, old_p)  20 us
    unnamed x2, waiting for transfers between devices  8.12 us
    all_to_all x1, starting transfers between devices, shards(): lax.all_to_all(send_counts, 'own', split_axis=0, concat_axis=0, tiled=True)  6.35 us
    reduce_sum x1, other arithmetic, shards(): square = jnp.sum(dense * dense)  6.14 us
    scatter-add x1, other arithmetic, shards(): dense = jax.ops.segment_sum(rows, target, num_segments=local_blocks)  5.23 us
    all_to_all x1, waiting for transfers between devices, shards(): lax.all_to_all(send_ids, 'own', split_axis=0, concat_axis=0, tiled=True)  5.21 us
  transfers between devices with their start and end apart: 4, of which 4 were waited for; matrix products, arithmetic and copies ran while one was open for 3% of the time, Pallas kernels for 0%

commit v1 on v0

v1 whole, which is shorter than its diff:
```python
import functools

import jax
import jax.numpy as jnp
from jax import lax
from jax.experimental import pallas as pl
from jax.experimental.pallas import tpu as pltpu
from jax.sharding import PartitionSpec as P

MESH = pl.DeviceIdType.MESH
HIGHEST = lax.Precision.HIGHEST
LANES = 128
PIECES = 4
ONE_M = 1.0 - 0.9**8
ONE_V = 1.0 - 0.99**8


def loop(count, body):
    if count <= 8:
        for i in range(count):
            body(i)
    else:

        def step(i, carry):
            body(i)
            return carry

        lax.fori_loop(0, count, step, 0)


def offset_of(i, n):
    return (n // 2 + ((i + 1) // 2) * (2 * (i % 2) - 1) + n) % n


def exchange_kernel(
    n_grp,
    n_own,
    slots,
    feats,
    grads,
    ids,
    counts,
    clip_out,
    keys_out,
    own_parts,
    got_parts,
    share,
    summed,
    key_send,
    key_got,
    dense,
    stat_send,
    stat_got,
    load_sem,
    part_send_sem,
    part_got_sem,
    share_send_sem,
    share_got_sem,
    key_send_sem,
    key_got_sem,
    stat_send_sem,
    stat_got_sem,
):
    my_g, my_o = lax.axis_index("grp"), lax.axis_index("own")
    n_dev = n_grp * n_own
    me = my_g * n_own + my_o
    per = slots * feats
    rows = n_own * per

    load = pltpu.make_async_copy(grads, own_parts, load_sem)
    load.start()
    barrier = pltpu.get_barrier_semaphore()

    def greet(i, carry):
        other = (me + 1 + i) % n_dev
        pl.semaphore_signal(
            barrier,
            inc=1,
            device_id={"grp": other // n_own, "own": other % n_own},
            device_id_type=MESH,
        )
        return carry

    lax.fori_loop(0, n_dev - 1, greet, 0)

    listing = ids[0, my_g].astype(jnp.float32)
    lane = lax.broadcasted_iota(jnp.int32, (slots, rows), 1)
    slot = lax.broadcasted_iota(jnp.int32, (slots, rows), 0)
    spread = jnp.where((lane % per) // feats == slot, 1.0, 0.0)
    wide = jnp.dot(listing, spread, precision=HIGHEST, preferred_element_type=jnp.float32)
    tally = counts[0, pl.ds(my_g, 1)].astype(jnp.float32)
    eye_r = lax.broadcasted_iota(jnp.int32, (n_own, n_own), 0)
    eye_c = lax.broadcasted_iota(jnp.int32, (n_own, n_own), 1)
    used = jnp.sum(jnp.where(eye_r == eye_c, jnp.broadcast_to(tally, (n_own, n_own)), 0.0), axis=1, keepdims=True)
    lane = lax.broadcasted_iota(jnp.int32, (n_own, rows), 1)
    number = ((lane % per) // feats).astype(jnp.float32)
    feature = (lane % feats).astype(jnp.float32)
    wide = jnp.where(number < used, jnp.round(wide) * feats + feature, -1.0)
    for o in range(n_own):
        key_send[o] = wide[o : o + 1]

    pl.semaphore_wait(barrier, n_dev - 1)

    def part_copy(i, hop):
        dest = (my_o + offset_of(i, n_own)) % n_own
        other = (my_g + hop + 1) % n_grp
        return pltpu.make_async_remote_copy(
            src_ref=own_parts.at[other, dest],
            dst_ref=got_parts.at[hop, dest],
            send_sem=part_send_sem.at[hop, i],
            recv_sem=part_got_sem.at[hop, i],
            device_id={"grp": other, "own": my_o},
            device_id_type=MESH,
        )

    def share_copy(i):
        dest = (my_o + offset_of(i, n_own)) % n_own
        return pltpu.make_async_remote_copy(
            src_ref=share.at[dest],
            dst_ref=summed.at[my_o],
            send_sem=share_send_sem.at[i],
            recv_sem=share_got_sem.at[i],
            device_id={"grp": my_g, "own": dest},
            device_id_type=MESH,
        )

    def key_copy(i):
        dest = (my_o + offset_of(i, n_own)) % n_own
        return pltpu.make_async_remote_copy(
            src_ref=key_send.at[dest],
            dst_ref=key_got.at[my_o],
            send_sem=key_send_sem.at[i],
            recv_sem=key_got_sem.at[i],
            device_id={"grp": my_g, "own": dest},
            device_id_type=MESH,
        )

    def stat_copy(i):
        other = (me + 1 + i) % n_dev
        return pltpu.make_async_remote_copy(
            src_ref=stat_send,
            dst_ref=stat_got.at[me],
            send_sem=stat_send_sem.at[i],
            recv_sem=stat_got_sem.at[i],
            device_id={"grp": other // n_own, "own": other % n_own},
            device_id_type=MESH,
        )

    load.wait()

    def send_parts(i):
        for hop in range(n_grp - 1):
            part_copy(i, hop).start()

    loop(n_own, send_parts)
    loop(n_own - 1, lambda i: key_copy(i).start())
    key_got[my_o] = key_send[my_o]

    def total_of(i):
        dest = (my_o + offset_of(i, n_own)) % n_own
        for hop in range(n_grp - 1):
            part_copy(i, hop).wait_recv()
        total = own_parts[my_g, dest]
        for hop in range(n_grp - 1):
            total = total + got_parts[hop, dest]
        return total

    def forward(i):
        dest = (my_o + offset_of(i, n_own)) % n_own
        share[dest] = total_of(i)
        share_copy(i).start()

    loop(n_own - 1, forward)
    summed[my_o] = total_of(n_own - 1)

    loop(n_own - 1, lambda i: key_copy(i).wait_recv())
    lane = lax.broadcasted_iota(jnp.int32, (n_own, rows), 1)
    source = lax.broadcasted_iota(jnp.int32, (n_own, rows), 0)
    keys = jnp.sum(jnp.where(lane // per == source, key_got[...].reshape(n_own, rows), 0.0), axis=0, keepdims=True)
    keys_out[...] = keys.astype(jnp.int32)
    tile = 256
    equals = []
    earlier = jnp.zeros((1, rows), jnp.float32)
    for b in range(rows // tile):
        column = jnp.transpose(jnp.broadcast_to(keys[:, b * tile : (b + 1) * tile], (LANES, tile)))
        column = jnp.concatenate([column] * (rows // LANES), axis=1)
        equal = jnp.where((column == keys) & (keys >= 0.0), 1.0, 0.0)
        down = lax.broadcasted_iota(jnp.int32, (tile, rows), 0) + b * tile
        right = lax.broadcasted_iota(jnp.int32, (tile, rows), 1)
        earlier = earlier + jnp.sum(jnp.where(down < right, equal, 0.0), axis=0, keepdims=True)
        equals.append(equal)
    first = jnp.where((earlier == 0.0) & (keys >= 0.0), 1.0, 0.0)

    loop(n_own - 1, lambda i: share_copy(i).wait_recv())
    slots_in = summed[...].reshape(rows, LANES)
    for b in range(rows // tile):
        dense[b * tile : (b + 1) * tile] = jnp.dot(
            equals[b], slots_in, precision=HIGHEST, preferred_element_type=jnp.float32
        )
    whole = dense[...]
    squares = jnp.dot(
        jnp.broadcast_to(first, (8, rows)), whole * whole, precision=HIGHEST, preferred_element_type=jnp.float32
    )
    square = jnp.sum(squares[0:1], axis=1, keepdims=True)
    touched = jnp.sum(first, axis=1, keepdims=True)
    spot = lax.broadcasted_iota(jnp.int32, (1, LANES), 1)
    stat = jnp.where(spot == 0, square, jnp.where(spot == 1, touched, 0.0))
    stat_send[...] = stat
    stat_got[me] = stat

    def send_stat(i, carry):
        stat_copy(i).start()
        return carry

    lax.fori_loop(0, n_dev - 1, send_stat, 0)

    def end_parts(i):
        for hop in range(n_grp - 1):
            part_copy(i, hop).wait_send()

    loop(n_own, end_parts)
    loop(n_own - 1, lambda i: key_copy(i).wait_send())
    loop(n_own - 1, lambda i: share_copy(i).wait_send())

    def get_stat(i, carry):
        stat_copy(i).wait_recv()
        return carry

    lax.fori_loop(0, n_dev - 1, get_stat, 0)
    stats = jnp.sum(stat_got[...].reshape(n_dev, LANES), axis=0, keepdims=True)
    square = jnp.sum(jnp.where(spot == 0, stats, 0.0), axis=1, keepdims=True)
    touched = jnp.sum(jnp.where(spot == 1, stats, 0.0), axis=1, keepdims=True)
    rms = jnp.sqrt(square / (touched * LANES) + 1e-06)
    scale = jnp.minimum(1.0, 0.5 / rms)
    clip_out[...] = scale * dense[...]

    def end_stat(i, carry):
        stat_copy(i).wait_send()
        return carry

    lax.fori_loop(0, n_dev - 1, end_stat, 0)


def update_kernel(
    feats, keys, clipped, old_p, old_m, old_v, new_p, new_m, new_v, p, m, v, rows_p, rows_m, rows_v, in_sem, out_sem
):
    total = p.shape[0]
    piece = total // PIECES
    trio = ((old_p, p, new_p), (old_m, m, new_m), (old_v, v, new_v))
    reads = []
    for a, (old, held, _) in enumerate(trio):
        for q in range(PIECES):
            part = pl.ds(q * piece, piece)
            reads.append(pltpu.make_async_copy(old.at[part], held.at[part], in_sem.at[a, q]))
    for read in reads:
        read.start()
    for read in reads:
        read.wait()
    count = clipped.shape[0] // feats

    def gather(t, carry):
        block = jnp.maximum(keys[0, t * feats], 0) // feats
        spot = pl.ds(t * feats, feats)
        rows_p[spot] = p[block]
        rows_m[spot] = m[block]
        rows_v[spot] = v[block]
        return carry

    lax.fori_loop(0, count, gather, 0, unroll=16)
    c = clipped[...]
    fresh_m = 0.9 * rows_m[...] + 0.1 * c
    fresh_v = 0.99 * rows_v[...] + 0.01 * c * c
    rows_p[...] = rows_p[...] - 0.01 * (fresh_m / ONE_M) / (jnp.sqrt(fresh_v / ONE_V) + 1e-08)
    rows_m[...] = fresh_m
    rows_v[...] = fresh_v

    writes = []
    for a, ((_, held, new), fresh) in enumerate(zip(trio, (rows_p, rows_m, rows_v))):

        def scatter(t, carry):
            key = keys[0, t * feats]

            @pl.when(key >= 0)
            def _():
                held[key // feats] = fresh[pl.ds(t * feats, feats)]

            return carry

        lax.fori_loop(0, count, scatter, 0, unroll=16)
        for q in range(PIECES):
            part = pl.ds(q * piece, piece)
            write = pltpu.make_async_copy(held.at[part], new.at[part], out_sem.at[a, q])
            write.start()
            writes.append(write)
    for write in writes:
        write.wait()


def shards(n_grp, n_own, grad_parts, block_ids, block_counts, params, first_moment, second_moment):
    slots, feats, width = grad_parts.shape[4:]
    per = slots * feats
    rows = n_own * per
    n_dev = n_grp * n_own
    f32 = jnp.float32
    vmem = pl.BlockSpec(memory_space=pltpu.VMEM)
    hbm = pl.BlockSpec(memory_space=pl.ANY)
    dma = pltpu.SemaphoreType.DMA
    clipped, keys = pl.pallas_call(
        functools.partial(exchange_kernel, n_grp, n_own, slots, feats),
        out_shape=(jax.ShapeDtypeStruct((rows, width), f32), jax.ShapeDtypeStruct((1, rows), jnp.int32)),
        in_specs=[hbm, vmem, vmem],
        out_specs=(vmem, vmem),
        scratch_shapes=[
            pltpu.VMEM((n_grp, n_own, per, width), f32),
            pltpu.VMEM((n_grp - 1, n_own, per, width), f32),
            pltpu.VMEM((n_own, per, width), f32),
            pltpu.VMEM((n_own, per, width), f32),
            pltpu.VMEM((n_own, 1, rows), f32),
            pltpu.VMEM((n_own, 1, rows), f32),
            pltpu.VMEM((rows, width), f32),
            pltpu.VMEM((1, LANES), f32),
            pltpu.VMEM((n_dev, 1, LANES), f32),
            dma,
            dma((n_grp - 1, n_own)),
            dma((n_grp - 1, n_own)),
            dma((n_own,)),
            dma((n_own,)),
            dma((n_own,)),
            dma((n_own,)),
            dma((n_dev,)),
            dma((n_dev,)),
        ],
        compiler_params=pltpu.CompilerParams(collective_id=0, has_side_effects=True),
        name="exchange",
    )(grad_parts.reshape(n_grp, n_own, per, width), block_ids, block_counts)

    shape = params.shape
    blocks = shape[0] * shape[1]
    table = jax.ShapeDtypeStruct((blocks, feats, width), f32)
    outs = pl.pallas_call(
        functools.partial(update_kernel, feats),
        out_shape=(table,) * 3,
        in_specs=[pl.BlockSpec(memory_space=pltpu.SMEM), vmem, hbm, hbm, hbm],
        out_specs=(hbm,) * 3,
        scratch_shapes=[pltpu.VMEM((blocks, feats, width), f32)] * 3
        + [pltpu.VMEM((rows, width), f32)] * 3
        + [dma((3, PIECES))] * 2,
        name="update",
    )(keys, clipped, *(x.reshape(blocks, feats, width) for x in (params, first_moment, second_moment)))
    return tuple(x.reshape(shape) for x in outs)


def solution(mesh):
    n_grp, n_own = mesh.shape["grp"], mesh.shape["own"]
    table = P(None, ("grp", "own"), None, None)
    return jax.shard_map(
        functools.partial(shards, n_grp, n_own),
        mesh=mesh,
        in_specs=(
            P("grp", "own", None, None, None, None, None),
            P("own", None, None, None),
            P("own", None, None),
            table,
            table,
            table,
        ),
        out_specs=(table, table, table),
        check_vma=False,
    )
```

time: 162 us -> 45.9 us (0.28)
  Pallas kernels: 0 us -> 45 us
  blocking collectives: 38.8 us -> 0 us
  local copies, waits for them, and re-layouts: 37 us -> 0 us
  other arithmetic: 34.2 us -> 0 us
  waiting for transfers between devices: 21.6 us -> 0 us
  between operations: 15.4 us -> 0.64 us
  starting transfers between devices: 14.3 us -> 0 us
    pallas_call x0 -> x2, Pallas kernels: none -> 45 us  [the longest x1 25.1 us: shards(): pl.pallas_call(functools.partial(exchange_kernel, n_grp, n_own, slots, fe...]
    psum x1 -> x0, blocking collectives: 38.8 us -> none  [shards(): square, touched = lax.psum((square, touched), ('grp', 'own'))]
    reshape x3 -> x0, local copies, waits for them, and re-layouts: 32.3 us -> none  [shards(): return (new_p.reshape(shape), new_m.reshape(shape), new_v.reshape(shape))]
    select_n x1 -> x0, other arithmetic: 20 us -> none  [shards(): new_p = jnp.where(mask, stepped, old_p)]
    all_to_all x3 -> x0, starting transfers between devices: 14.3 us -> none  [the longest x1 6.35 us: shards(): lax.all_to_all(send_counts, 'own', split_axis=0, concat_axis=0, tiled=True)]
    all_to_all x3 -> x0, waiting for transfers between devices: 13.5 us -> none  [the longest x1 5.21 us: shards(): lax.all_to_all(send_ids, 'own', split_axis=0, concat_axis=0, tiled=True)]
    unnamed x2 -> x0, waiting for transfers between devices: 8.12 us -> none
    reduce_sum x2 -> x0, other arithmetic: 6.75 us -> none  [the longest x1 6.14 us: shards(): square = jnp.sum(dense * dense)]
  transfers between devices with their start and end apart: 4 -> 0, of which waited for: 4 -> 0; matrix products, arithmetic and copies ran while one was open for 3% -> 0% of each run, Pallas kernels for 0% -> 0%
where the time goes in v1:
time: 45.9 us; the launch traced here: 45.6 us
  Pallas kernels  45 us (98%)
  between operations  0.64 us (1%)
    pallas_call x1, Pallas kernels, shards(): pl.pallas_call(functools.partial(exchange_kernel, n_grp, n_own, slots, fe...  25.1 us
    pallas_call x1, Pallas kernels, shards(): pl.pallas_call(functools.partial(update_kernel, feats), out_shape=(table,...  19.8 us

profile of v1, /device:TPU:0, one launch (start us, length us, event | category | flops | bytes accessed | tf_op | source)
XLA Modules:
  0.0 45.6 jit_solution(152099813606332855)
XLA Ops:
  0.6 25.1 %exchange.1 = (f32[256,128]{1,0:T(8,128)}, s32[1,256]{1,0:T(1,128)}) custom-call(f32[4,8,32,128]{3,2,1,0:T(8,128)} %bitcast.10, s32[1,4,8,16]{3,2,1,0:T(8,128)} %ids.1, s32[1,4,8]{2,1,0:T(4,128)} %counts.1), custom_call_target="tpu_custom_call" | custom-call | tf_op jit(solution)/shard_map/exchange/pallas_call | solution.py:308
  25.8 19.8 %update.1 = (f32[8192,2,128]{2,1,0:T(2,128)}, f32[8192,2,128]{2,1,0:T(2,128)}, f32[8192,2,128]{2,1,0:T(2,128)}) custom-call(s32[1,256]{1,0:T(1,128)} %get-tuple-element.8.keys, f32[256,128]{1,0:T(8,128)} %get-tuple-element.9.clipped, f32[8192,2,128]{2,1,0:T(2,128)} %bitcast.7, f32[8192,2,128]{2,1,0:T(2,128)} %bitcast.8, f32[8192,2,128]{2,1,0:T(2,128)} %bitcast.9), custom_call_target="tpu_custom_call" | custom-call | tf_op jit(solution)/shard_map/update/pallas_call | solution.py:340

commit v2 on v1

--- a/solution.py
+++ b/solution.py
@@ -11,6 +11,8 @@
 HIGHEST = lax.Precision.HIGHEST
 LANES = 128
 PIECES = 4
+EXCHANGE_VMEM = 32 << 20
+WRITE_VMEM = 2 << 20
 ONE_M = 1.0 - 0.9**8
 ONE_V = 1.0 - 0.99**8
 
@@ -40,8 +42,16 @@
     grads,
     ids,
     counts,
-    clip_out,
+    old_p,
+    old_m,
+    old_v,
     keys_out,
+    rows_p,
+    rows_m,
+    rows_v,
+    held_p,
+    held_m,
+    held_v,
     own_parts,
     got_parts,
     share,
@@ -51,7 +61,10 @@
     dense,
     stat_send,
     stat_got,
+    key_scalars,
     load_sem,
+    table_sem,
+    scalar_sem,
     part_send_sem,
     part_got_sem,
     share_send_sem,
@@ -69,6 +82,12 @@
 
     load = pltpu.make_async_copy(grads, own_parts, load_sem)
     load.start()
+    piece = old_p.shape[0] // PIECES
+    reads = []
+    for a, (old, held) in enumerate(((old_p, held_p), (old_m, held_m), (old_v, held_v))):
+        for q in range(PIECES):
+            part = pl.ds(q * piece, piece)
+            reads.append(pltpu.make_async_copy(old.at[part], held.at[part], table_sem.at[a, q]))
     barrier = pltpu.get_barrier_semaphore()
 
     def greet(i, carry):
@@ -83,19 +102,17 @@
 
     lax.fori_loop(0, n_dev - 1, greet, 0)
 
-    listing = ids[0, my_g].astype(jnp.float32)
-    lane = lax.broadcasted_iota(jnp.int32, (slots, rows), 1)
-    slot = lax.broadcasted_iota(jnp.int32, (slots, rows), 0)
-    spread = jnp.where((lane % per) // feats == slot, 1.0, 0.0)
-    wide = jnp.dot(listing, spread, precision=HIGHEST, preferred_element_type=jnp.float32)
-    tally = counts[0, pl.ds(my_g, 1)].astype(jnp.float32)
+    listing = ids[0, my_g]
+    lane = lax.broadcasted_iota(jnp.int32, (n_own, rows), 1)
+    number = (lane % per) // feats
+    wide = jnp.broadcast_to(listing[:, 0:1], (n_own, rows))
+    for j in range(1, slots):
+        wide = jnp.where(number == j, listing[:, j : j + 1], wide)
+    tally = counts[0, pl.ds(my_g, 1)]
     eye_r = lax.broadcasted_iota(jnp.int32, (n_own, n_own), 0)
     eye_c = lax.broadcasted_iota(jnp.int32, (n_own, n_own), 1)
-    used = jnp.sum(jnp.where(eye_r == eye_c, jnp.broadcast_to(tally, (n_own, n_own)), 0.0), axis=1, keepdims=True)
-    lane = lax.broadcasted_iota(jnp.int32, (n_own, rows), 1)
-    number = ((lane % per) // feats).astype(jnp.float32)
-    feature = (lane % feats).astype(jnp.float32)
-    wide = jnp.where(number < used, jnp.round(wide) * feats + feature, -1.0)
+    used = jnp.sum(jnp.where(eye_r == eye_c, jnp.broadcast_to(tally, (n_own, n_own)), 0), axis=1, keepdims=True)
+    wide = jnp.where(number < used, wide * feats + lane % feats, -1)
     for o in range(n_own):
         key_send[o] = wide[o : o + 1]
 
@@ -147,6 +164,8 @@
         )
 
     load.wait()
+    for read in reads:
+        read.start()
 
     def send_parts(i):
         for hop in range(n_grp - 1):
@@ -176,20 +195,22 @@
     loop(n_own - 1, lambda i: key_copy(i).wait_recv())
     lane = lax.broadcasted_iota(jnp.int32, (n_own, rows), 1)
     source = lax.broadcasted_iota(jnp.int32, (n_own, rows), 0)
-    keys = jnp.sum(jnp.where(lane // per == source, key_got[...].reshape(n_own, rows), 0.0), axis=0, keepdims=True)
-    keys_out[...] = keys.astype(jnp.int32)
+    keys = jnp.sum(jnp.where(lane // per == source, key_got[...].reshape(n_own, rows), 0), axis=0, keepdims=True)
+    keys_out[...] = keys
+    to_scalars = pltpu.make_async_copy(keys_out, key_scalars, scalar_sem)
+    to_scalars.start()
     tile = 256
     equals = []
     earlier = jnp.zeros((1, rows), jnp.float32)
     for b in range(rows // tile):
         column = jnp.transpose(jnp.broadcast_to(keys[:, b * tile : (b + 1) * tile], (LANES, tile)))
         column = jnp.concatenate([column] * (rows // LANES), axis=1)
-        equal = jnp.where((column == keys) & (keys >= 0.0), 1.0, 0.0)
+        equal = jnp.where((column == keys) & (keys >= 0), 1.0, 0.0)
         down = lax.broadcasted_iota(jnp.int32, (tile, rows), 0) + b * tile
         right = lax.broadcasted_iota(jnp.int32, (tile, rows), 1)
         earlier = earlier + jnp.sum(jnp.where(down < right, equal, 0.0), axis=0, keepdims=True)
         equals.append(equal)
-    first = jnp.where((earlier == 0.0) & (keys >= 0.0), 1.0, 0.0)
+    first = jnp.where((earlier == 0.0) & (keys >= 0), 1.0, 0.0)
 
     loop(n_own - 1, lambda i: share_copy(i).wait_recv())
     slots_in = summed[...].reshape(rows, LANES)
@@ -222,6 +243,20 @@
     loop(n_own - 1, lambda i: key_copy(i).wait_send())
     loop(n_own - 1, lambda i: share_copy(i).wait_send())
 
+    to_scalars.wait()
+    for read in reads:
+        read.wait()
+
+    def gather(t, carry):
+        block = jnp.clip(key_scalars[0, t * feats] // feats, 0, held_p.shape[0] - 1)
+        spot = pl.ds(t * feats, feats)
+        rows_p[spot] = held_p[block]
+        rows_m[spot] = held_m[block]
+        rows_v[spot] = held_v[block]
+        return carry
+
+    lax.fori_loop(0, rows // feats, gather, 0, unroll=16)
+
     def get_stat(i, carry):
         stat_copy(i).wait_recv()
         return carry
@@ -232,50 +267,25 @@
     touched = jnp.sum(jnp.where(spot == 1, stats, 0.0), axis=1, keepdims=True)
     rms = jnp.sqrt(square / (touched * LANES) + 1e-06)
     scale = jnp.minimum(1.0, 0.5 / rms)
-    clip_out[...] = scale * dense[...]
-
-    def end_stat(i, carry):
-        stat_copy(i).wait_send()
-        return carry
-
-    lax.fori_loop(0, n_dev - 1, end_stat, 0)
-
-
-def update_kernel(
-    feats, keys, clipped, old_p, old_m, old_v, new_p, new_m, new_v, p, m, v, rows_p, rows_m, rows_v, in_sem, out_sem
-):
-    total = p.shape[0]
-    piece = total // PIECES
-    trio = ((old_p, p, new_p), (old_m, m, new_m), (old_v, v, new_v))
-    reads = []
-    for a, (old, held, _) in enumerate(trio):
-        for q in range(PIECES):
-            part = pl.ds(q * piece, piece)
-            reads.append(pltpu.make_async_copy(old.at[part], held.at[part], in_sem.at[a, q]))
-    for read in reads:
-        read.start()
-    for read in reads:
-        read.wait()
-    count = clipped.shape[0] // feats
-
-    def gather(t, carry):
-        block = jnp.maximum(keys[0, t * feats], 0) // feats
-        spot = pl.ds(t * feats, feats)
-        rows_p[spot] = p[block]
-        rows_m[spot] = m[block]
-        rows_v[spot] = v[block]
-        return carry
-
-    lax.fori_loop(0, count, gather, 0, unroll=16)
-    c = clipped[...]
-    fresh_m = 0.9 * rows_m[...] + 0.1 * c
-    fresh_v = 0.99 * rows_v[...] + 0.01 * c * c
+    clipped = scale * dense[...]
+    fresh_m = 0.9 * rows_m[...] + 0.1 * clipped
+    fresh_v = 0.99 * rows_v[...] + 0.01 * clipped * clipped
     rows_p[...] = rows_p[...] - 0.01 * (fresh_m / ONE_M) / (jnp.sqrt(fresh_v / ONE_V) + 1e-08)
     rows_m[...] = fresh_m
     rows_v[...] = fresh_v
 
+    def end_stat(i, carry):
+        stat_copy(i).wait_send()
+        return carry
+
+    lax.fori_loop(0, n_dev - 1, end_stat, 0)
+
+
+def write_kernel(feats, keys, rows_p, rows_m, rows_v, old_p, old_m, old_v, p, m, v, new_p, new_m, new_v, sem):
+    piece = p.shape[0] // PIECES
+    count = rows_p.shape[0] // feats
     writes = []
-    for a, ((_, held, new), fresh) in enumerate(zip(trio, (rows_p, rows_m, rows_v))):
+    for a, (fresh, held, new) in enumerate(((rows_p, p, new_p), (rows_m, m, new_m), (rows_v, v, new_v))):
 
         def scatter(t, carry):
             key = keys[0, t * feats]
@@ -289,7 +299,7 @@
         lax.fori_loop(0, count, scatter, 0, unroll=16)
         for q in range(PIECES):
             part = pl.ds(q * piece, piece)
-            write = pltpu.make_async_copy(held.at[part], new.at[part], out_sem.at[a, q])
+            write = pltpu.make_async_copy(held.at[part], new.at[part], sem.at[a, q])
             write.start()
             writes.append(write)
     for write in writes:
@@ -305,21 +315,29 @@
     vmem = pl.BlockSpec(memory_space=pltpu.VMEM)
     hbm = pl.BlockSpec(memory_space=pl.ANY)
     dma = pltpu.SemaphoreType.DMA
-    clipped, keys = pl.pallas_call(
+    shape = params.shape
+    blocks = shape[0] * shape[1]
+    table = (blocks, feats, width)
+    keys, rows_p, rows_m, rows_v, *held = pl.pallas_call(
         functools.partial(exchange_kernel, n_grp, n_own, slots, feats),
-        out_shape=(jax.ShapeDtypeStruct((rows, width), f32), jax.ShapeDtypeStruct((1, rows), jnp.int32)),
-        in_specs=[hbm, vmem, vmem],
-        out_specs=(vmem, vmem),
+        out_shape=(pltpu.VMEM((1, rows), jnp.int32),)
+        + (pltpu.VMEM((rows, width), f32),) * 3
+        + (pltpu.VMEM(table, f32),) * 3,
+        in_specs=[hbm, vmem, vmem, hbm, hbm, hbm],
+        out_specs=(vmem,) * 7,
         scratch_shapes=[
             pltpu.VMEM((n_grp, n_own, per, width), f32),
             pltpu.VMEM((n_grp - 1, n_own, per, width), f32),
             pltpu.VMEM((n_own, per, width), f32),
             pltpu.VMEM((n_own, per, width), f32),
-            pltpu.VMEM((n_own, 1, rows), f32),
-            pltpu.VMEM((n_own, 1, rows), f32),
+            pltpu.VMEM((n_own, 1, rows), jnp.int32),
+            pltpu.VMEM((n_own, 1, rows), jnp.int32),
             pltpu.VMEM((rows, width), f32),
             pltpu.VMEM((1, LANES), f32),
             pltpu.VMEM((n_dev, 1, LANES), f32),
+            pltpu.SMEM((1, rows), jnp.int32),
+            dma,
+            dma((3, PIECES)),
             dma,
             dma((n_grp - 1, n_own)),
             dma((n_grp - 1, n_own)),
@@ -330,24 +348,28 @@
             dma((n_dev,)),
             dma((n_dev,)),
         ],
-        compiler_params=pltpu.CompilerParams(collective_id=0, has_side_effects=True),
+        compiler_params=pltpu.CompilerParams(
+            collective_id=0, has_side_effects=True, vmem_limit_bytes=EXCHANGE_VMEM
+        ),
         name="exchange",
-    )(grad_parts.reshape(n_grp, n_own, per, width), block_ids, block_counts)
-
-    shape = params.shape
-    blocks = shape[0] * shape[1]
-    table = jax.ShapeDtypeStruct((blocks, feats, width), f32)
+    )(
+        grad_parts.reshape(n_grp, n_own, per, width),
+        block_ids,
+        block_counts,
+        *(pltpu.with_memory_space_constraint(x.reshape(table), pltpu.HBM) for x in (params, first_moment, second_moment)),
+    )
+
     outs = pl.pallas_call(
-        functools.partial(update_kernel, feats),
-        out_shape=(table,) * 3,
-        in_specs=[pl.BlockSpec(memory_space=pltpu.SMEM), vmem, hbm, hbm, hbm],
-        out_specs=(hbm,) * 3,
-        scratch_shapes=[pltpu.VMEM((blocks, feats, width), f32)] * 3
-        + [pltpu.VMEM((rows, width), f32)] * 3
-        + [dma((3, PIECES))] * 2,
-        name="update",
-    )(keys, clipped, *(x.reshape(blocks, feats, width) for x in (params, first_moment, second_moment)))
-    return tuple(x.reshape(shape) for x in outs)
+        functools.partial(write_kernel, feats),
+        out_shape=(pltpu.VMEM(table, f32),) * 3 + (jax.ShapeDtypeStruct(table, f32),) * 3,
+        in_specs=[pl.BlockSpec(memory_space=pltpu.SMEM)] + [vmem] * 6,
+        out_specs=(vmem,) * 3 + (pl.BlockSpec(memory_space=pltpu.HBM),) * 3,
+        input_output_aliases={4: 0, 5: 1, 6: 2},
+        scratch_shapes=[dma((3, PIECES))],
+        compiler_params=pltpu.CompilerParams(vmem_limit_bytes=WRITE_VMEM),
+        name="write",
+    )(keys, rows_p, rows_m, rows_v, *held)
+    return tuple(x.reshape(shape) for x in outs[3:])
 
 
 def solution(mesh):

time: 45.9 us -> 36.1 us (0.79)
  Pallas kernels: 45 us -> 35.3 us
    pallas_call x1, Pallas kernels: 19.8 us -> 10.5 us  [shards(): pl.pallas_call(functools.partial(write_kernel, feats), out_shape=(pltpu.V...]
where the time goes in v2:
time: 36.1 us; the launch traced here: 35.9 us
  Pallas kernels  35.3 us (98%)
  between operations  0.64 us (2%)
    pallas_call x1, Pallas kernels, shards(): pl.pallas_call(functools.partial(exchange_kernel, n_grp, n_own, slots, fe...  24.7 us
    pallas_call x1, Pallas kernels, shards(): pl.pallas_call(functools.partial(write_kernel, feats), out_shape=(pltpu.V...  10.5 us

profile of v2, /device:TPU:0, one launch (start us, length us, event | category | flops | bytes accessed | tf_op | source)
XLA Modules:
  0.0 35.9 jit_solution(6763304170778198538)
XLA Ops:
  0.6 24.7 %exchange.1 = (s32[1,256]{1,0:T(1,128)S(1)}, f32[256,128]{1,0:T(8,128)S(1)}, f32[256,128]{1,0:T(8,128)S(1)}, f32[256,128]{1,0:T(8,128)S(1)}, f32[8192,2,128]{2,1...) custom-call(f32[4,8,32,128]{3,2,1,0:T(8,128)} %bitcast.10, s32[1,4,8,16]{3,2,1,0:T(8,128)} %ids.1, ...), custom_call_target="tpu_custom_call" | custom-call | tf_op jit(solution)/shard_map/exchange/pallas_call | solution.py:321
  25.4 10.5 %write.1 = (f32[8192,2,128]{2,1,0:T(2,128)S(1)}, f32[8192,2,128]{2,1,0:T(2,128)S(1)}, f32[8192,2,128]{2,1,0:T(2,128)S(1)}, f32[8192,2,128]{2,1,0:T(2,128)}, f32[...) custom-call(s32[1,256]{1,0:T(1,128)S(1)} %get-tuple-element.13.keys, ...), custom_call_target="tpu_custom_call", output_to_operand_aliasing={{0}: (4, {}), {1}: (5, {}), {2}: (6, {})} | custom-call | tf_op jit(solution)/shard_map/write/pallas_call | solution.py:362
